TPU v7x, 32 devices: a whole 2x2x4 slice. The times are simulated.
32 devices in a mesh: clients: 8 (over z, x), shard: 4 (over y, core).
Axes of the slice: x: 2, y: 2, z: 4, core: 2. Of those that a mesh axis runs over, the one named last changes fastest.
Arguments:
- quantized: int32 [8, 2097152], P('clients', 'shard'), may hold values from 0 to 2097151
- pair_masks: int32 [8, 2097152], P('clients', 'shard'), may hold values from 0 to 2097142, as said below
- alive_flags: int32 [8], P('clients'), may hold values from 0 to 1, as said below
- row_seeds: int32 [64], replicated, may hold values from 0 to 1073741823
Outputs:
- aggregate: int32 [2097152], P('shard')
- commitments: int32 [8, 64], P('clients')
- mismatch: int32 [64], replicated
Inputs may be any that keep to these rules, and one draw needn't show every extreme that they name: For every position, the pair_masks of all 8 participants sum to a multiple of 2097143. `alive_flags`: at least one participant has flag 1 and at least one has flag 0.
All inputs are finite; a program needn't handle non-finite values.
Results may differ from a plain program's by a relative error of at most 0.000001.
Values may be sent and summed in bfloat16 or wider, within the bound.
A program may use at most 64 MiB of HBM per device.

v0:
```python
import functools

import jax
import jax.numpy as jnp
from jax import lax
from jax.experimental import pallas as pl
from jax.experimental.pallas import tpu as pltpu
from jax.sharding import PartitionSpec as P

modulus = 2097143
LANES = 128
GROUP = 16
STRIDE = (LANES * 747796405 + 2147483648) % 4294967296 - 2147483648


def reduce_mod(x):
    x = (x & 2097151) + (x >> 21) * 9
    return jnp.where(x >= modulus, x - modulus, x)


def table_tile(start):
    v = start & 2147483647
    v = v ^ (v >> 15)
    v = (v * 277803737) & 2147483647
    v = v ^ (v >> 13)
    v = v * 1103515245
    v = v ^ (v >> 16)
    high = (v & 992).astype(jnp.float32).astype(jnp.bfloat16)
    low = (v & 31).astype(jnp.float32).astype(jnp.bfloat16)
    return high, low


def aggregate_kernel(
    clients,
    length,
    alive_ref,
    seeds_ref,
    quant_ref,
    masks_ref,
    agg_out,
    own_out,
    diff_out,
    masked,
    arrived,
    agg,
    base,
    tables,
    pieces,
    send_sem,
    recv_sem,
    out_sem,
    own_parts,
    diff_parts,
    own_send,
    own_recv,
    diff_send,
    diff_recv,
    partner_q,
    swap_send,
    swap_recv,
):
    rows = quant_ref.shape[0]
    half = rows // 2
    checks = seeds_ref.shape[0]
    bits = clients.bit_length() - 1
    me = lax.axis_index("clients")
    shards = lax.axis_size("shard")
    here = lax.axis_index("shard")
    start = lax.axis_index("shard") * length
    alive = alive_ref[0]

    barrier = pltpu.get_barrier_semaphore()
    for n in range(1, clients):
        pl.semaphore_signal(barrier, inc=1, device_id={"clients": me ^ n})
    for n in range(1, shards):
        there = lax.rem(here + n, shards)
        pl.semaphore_signal(barrier, inc=1, device_id={"shard": there})
        pl.semaphore_signal(barrier, inc=1, device_id={"shard": there, "clients": me ^ 1})
    peers = clients + 2 * shards - 3

    def mask_rows(lo, count):
        step = min(64, count)

        @pl.loop(0, count // step)
        def _(i):
            at = pl.ds(pl.multiple_of(lo + i * step, 8), step)
            s = quant_ref[at, :] + masks_ref[at, :]
            s = jnp.where(s >= modulus, s - modulus, s)
            s = jnp.where(s >= modulus, s - modulus, s)
            masked[at, :] = s * alive

    plans = []
    for h in range(2):
        order = list(range(bits))
        if h == 1:
            order = order[1:] + order[:1]
        lo = h * half
        count = half
        landing = h * half
        scatter, gather = [], []
        for n, b in enumerate(order):
            count //= 2
            bit = (me >> b) & 1
            keep = pl.multiple_of(lo + bit * count, 8)
            give = pl.multiple_of(lo + (1 - bit) * count, 8)
            scatter.append((b, keep, give, count, landing, n))
            gather.append((b, keep, give, count, n))
            landing += count
            lo = keep
        plans.append((scatter, gather[::-1], lo, count))

    def scatter_copy(h, n):
        b, keep, give, count, landing, _ = plans[h][0][n]
        return pltpu.make_async_remote_copy(
            src_ref=masked.at[pl.ds(give, count)],
            dst_ref=arrived.at[pl.ds(landing, count)],
            send_sem=send_sem.at[h, n],
            recv_sem=recv_sem.at[h, n],
            device_id={"clients": me ^ (1 << b)},
        )

    def gather_copy(h, n):
        b, keep, give, count, _ = plans[h][1][n]
        return pltpu.make_async_remote_copy(
            src_ref=agg.at[pl.ds(keep, count)],
            dst_ref=agg.at[pl.ds(keep, count)],
            send_sem=send_sem.at[h, bits + n],
            recv_sem=recv_sem.at[h, bits + n],
            device_id={"clients": me ^ (1 << b)},
        )

    def gather_wait(h, n):
        b, keep, give, count, _ = plans[h][1][n]
        gather_copy(h, n).wait_send()
        pltpu.make_async_remote_copy(
            src_ref=agg.at[pl.ds(give, count)],
            dst_ref=agg.at[pl.ds(give, count)],
            send_sem=send_sem.at[h, bits + n],
            recv_sem=recv_sem.at[h, bits + n],
            device_id={"clients": me ^ (1 << b)},
        ).wait_recv()

    def add_arrived(h, n):
        _, keep, _, count, landing, _ = plans[h][0][n]
        step = min(64, count)
        last = n == bits - 1

        @pl.loop(0, count // step)
        def _(i):
            at = pl.ds(pl.multiple_of(keep + i * step, 8), step)
            got = pl.ds(pl.multiple_of(landing + i * step, 8), step)
            s = masked[at, :] + arrived[got, :]
            if last:
                agg[at, :] = reduce_mod(s)
            else:
                masked[at, :] = s

    block = half // clients
    shares = [plans[0][2] // block, (plans[1][2] - half) // block]
    unit = 2 * GROUP
    per_block = block // unit
    others = clients // 2 - 1

    def block_row(h, k, flip=0):
        if h == 0:
            return (shares[0] ^ (k + flip * (clients // 2))) * block
        return half + (shares[1] ^ (2 * k + flip)) * block

    work = [(h, k) for h in range(2) for k in range(others, 0, -1)] + [(0, 0), (1, 0)]

    def swap_copy(n):
        at = pl.multiple_of(block_row(*work[n], 1), 8)
        return pltpu.make_async_remote_copy(
            src_ref=quant_ref.at[pl.ds(at, block)],
            dst_ref=partner_q.at[pl.ds(at, block)],
            send_sem=swap_send.at[n],
            recv_sem=swap_recv.at[n],
            device_id={"clients": me ^ 1},
        )

    def swap_wait(n):
        swap_copy(n).wait_send()
        at = pl.multiple_of(block_row(*work[n]), 8)
        pltpu.make_async_remote_copy(
            src_ref=partner_q.at[pl.ds(at, block)],
            dst_ref=partner_q.at[pl.ds(at, block)],
            send_sem=swap_send.at[n],
            recv_sem=swap_recv.at[n],
            device_id={"clients": me ^ 1},
        ).wait_recv()

    def pair_row(u, share):
        each = per_block if share else others * per_block
        r = u - (0 if not share else 2 * others * per_block)
        h = (r >= each).astype(jnp.int32)
        r = r - h * each
        k = 0 if share else others - r // per_block
        a = (shares[0] ^ k) * block
        b = half + (shares[1] ^ (2 * k)) * block
        row = jnp.where(h == 1, b, a) + (r % per_block) * unit
        return pl.multiple_of(row, unit)

    early = min(2, len(work))
    pl.semaphore_wait(barrier, peers)
    for n in range(early):
        swap_copy(n).start()
    for h in (1, 0):
        _, keep, give, count, _, _ = plans[h][0][0]
        mask_rows(give, count)
    lane = lax.broadcasted_iota(jnp.int32, (checks, LANES), 1)
    base[...] = (lane + start) * 747796405 + seeds_ref[...]
    tables[1] = jnp.zeros_like(tables[1])
    pieces[1] = jnp.zeros_like(pieces[1])
    for h in (1, 0):
        scatter_copy(h, 0).start()
    for n in range(early, len(work)):
        swap_copy(n).start()
    for h in range(2):
        _, keep, give, count, _, _ = plans[h][0][0]
        mask_rows(keep, count)

    sub = lax.broadcasted_iota(jnp.int32, (8, LANES), 0)
    empty = jnp.zeros((8, LANES), jnp.float32)
    shift = 7 * (sub & 3)
    second = sub >= 4

    def pending(slot, total):
        part = lax.dot_general(
            pieces[slot], tables[slot], (((1,), (1,)), ((), ())), preferred_element_type=jnp.float32
        )
        return reduce_mod(total + part.astype(jnp.int32))

    def fill(slot, row, share):
        for k in range(GROUP):
            at = row + k
            high, low = table_tile(base[...] + at * STRIDE)
            cols = pl.ds(k * LANES, LANES)
            tables[slot, :checks, cols] = high
            tables[slot, checks:, cols] = low
            one = jnp.broadcast_to(quant_ref[pl.ds(at, 1), :], (8, LANES))
            two = jnp.broadcast_to(partner_q[pl.ds(at, 1), :], (8, LANES))
            both = ((jnp.where(second, two, one) >> shift) & 127).astype(jnp.float32)
            if share:
                three = jnp.broadcast_to(agg[pl.ds(at, 1), :], (8, LANES))
                third = jnp.where(second, 0, (three >> shift) & 127).astype(jnp.float32)
            else:
                third = empty
            both = jnp.concatenate([both, third], 0)
            pieces[slot, :, cols] = both.astype(jnp.bfloat16)

    def compute(first, last, share, total):
        def pair(u, total):
            row = pair_row(u, share)
            total = pending(1, total)
            fill(0, row, share)
            total = pending(0, total)
            fill(1, row + GROUP, share)
            return total

        return lax.fori_loop(first, last, pair, total)

    actions = []
    for n in range(bits):
        for h in (1, 0):
            def take(h=h, n=n):
                scatter_copy(h, n).wait()
                add_arrived(h, n)

            def send(h=h, n=n):
                if n < bits - 1:
                    scatter_copy(h, n + 1).start()
                else:
                    gather_copy(h, 0).start()

            actions.append((take, send))
    for n in range(bits):
        for h in (1, 0):
            def take(h=h, n=n):
                gather_wait(h, n)

            def send(h=h, n=n):
                if n < bits - 1:
                    gather_copy(h, n + 1).start()

            actions.append((take, send))

    pairs = rows // 2 // unit
    shared_from = 2 * others * per_block
    early_part = pairs * 11 // 16
    stops = [early_part * (i + 1) // (2 * bits) for i in range(2 * bits)]
    stops += [
        early_part + (pairs - early_part) * (i + 1) // (2 * bits) for i in range(2 * bits)
    ]
    done, swapped = 0, 0
    total = jnp.zeros((16, LANES), jnp.int32)
    for until, (take, send) in zip(stops, actions):
        while swapped * per_block < until:
            swap_wait(swapped)
            swapped += 1
        if done < min(until, shared_from):
            total = compute(done, min(until, shared_from), False, total)
        if max(done, shared_from) < until:
            total = compute(max(done, shared_from), until, True, total)
        done = until
        take()
        send()
    store = pltpu.make_async_copy(agg, agg_out, out_sem)
    store.start()
    total = pending(1, total)

    own_parts[0] = total
    own_copies = []
    for n in range(1, 2 * shards):
        where = {"shard": lax.rem(here + n % shards, shards)} if n % shards else {}
        if n >= shards:
            where["clients"] = me ^ 1
        own_copies.append(
            pltpu.make_async_remote_copy(
                src_ref=own_parts.at[0],
                dst_ref=own_parts.at[n],
                send_sem=own_send.at[n],
                recv_sem=own_recv.at[n],
                device_id=where,
            )
        )
    for copy in own_copies:
        copy.start()
    for copy in own_copies:
        copy.wait()
    mine, theirs = own_parts[0], own_parts[shards]
    for n in range(1, shards):
        mine = mine + own_parts[n]
        theirs = theirs + own_parts[shards + n]
    total = reduce_mod(mine[:8] + pltpu.roll(theirs[:8], 4, 0))
    own_out[...] = total
    diff = reduce_mod(mine[8:]) - total * alive
    diff = jnp.where(diff < 0, diff + modulus, diff)
    diff_parts[0] = diff
    diff_copies = [
        pltpu.make_async_remote_copy(
            src_ref=diff_parts.at[0],
            dst_ref=diff_parts.at[n],
            send_sem=diff_send.at[n],
            recv_sem=diff_recv.at[n],
            device_id={"clients": me ^ n},
        )
        for n in range(1, clients)
    ]
    for copy in diff_copies:
        copy.start()
    for copy in diff_copies:
        copy.wait()
    for n in range(1, clients):
        diff = diff + diff_parts[n]
    diff_out[...] = reduce_mod(diff)
    store.wait()


def aggregate_and_project(quantized, pair_masks, alive_flags, row_seeds, clients, shards):
    length = quantized.shape[1]
    rows = length // LANES
    checks = row_seeds.shape[0]
    bits = clients.bit_length() - 1
    vmem = pl.BlockSpec(memory_space=pltpu.VMEM)
    return pl.pallas_call(
        functools.partial(aggregate_kernel, clients, length),
        in_specs=[pl.BlockSpec(memory_space=pltpu.SMEM), vmem, vmem, vmem],
        out_specs=[pl.BlockSpec(memory_space=pl.ANY), vmem, vmem],
        out_shape=[
            jax.ShapeDtypeStruct((rows, LANES), jnp.int32),
            jax.ShapeDtypeStruct((8, 2 * checks), jnp.int32),
            jax.ShapeDtypeStruct((8, 2 * checks), jnp.int32),
        ],
        scratch_shapes=[
            pltpu.VMEM((rows, LANES), jnp.int32),
            pltpu.VMEM((rows, LANES), jnp.int32),
            pltpu.VMEM((rows, LANES), jnp.int32),
            pltpu.VMEM((checks, LANES), jnp.int32),
            pltpu.VMEM((2, 2 * checks, GROUP * LANES), jnp.bfloat16),
            pltpu.VMEM((2, 16, GROUP * LANES), jnp.bfloat16),
            pltpu.SemaphoreType.DMA((2, 2 * bits)),
            pltpu.SemaphoreType.DMA((2, 2 * bits)),
            pltpu.SemaphoreType.DMA,
            pltpu.VMEM((2 * shards, 16, 2 * checks), jnp.int32),
            pltpu.VMEM((clients, 8, 2 * checks), jnp.int32),
            pltpu.SemaphoreType.DMA((2 * shards,)),
            pltpu.SemaphoreType.DMA((2 * shards,)),
            pltpu.SemaphoreType.DMA((clients,)),
            pltpu.SemaphoreType.DMA((clients,)),
            pltpu.VMEM((rows, LANES), jnp.int32),
            pltpu.SemaphoreType.DMA((clients,)),
            pltpu.SemaphoreType.DMA((clients,)),
        ],
        compiler_params=pltpu.CompilerParams(collective_id=0, has_side_effects=True),
        name="aggregate_and_project",
    )(
        alive_flags,
        row_seeds[:, None],
        quantized.reshape(rows, LANES),
        pair_masks.reshape(rows, LANES),
    )


def checksum(parts):
    checks = parts.shape[1] // 2
    parts = reduce_mod(parts[:, :checks] + parts[:, checks:])
    return reduce_mod(reduce_mod(parts[2] * 128 + parts[1]) * 128 + parts[0])


def body(quantized, pair_masks, alive_flags, row_seeds):
    length = quantized.shape[1]
    clients = lax.axis_size("clients")
    shards = lax.axis_size("shard")
    aggregate, own, diff = aggregate_and_project(
        quantized, pair_masks, alive_flags, row_seeds, clients, shards
    )
    return (aggregate.reshape(length), checksum(own)[None, :], checksum(diff))


def solution(mesh):
    placed = (P("clients", "shard"), P("clients", "shard"), P("clients"), P())
    return jax.shard_map(
        body,
        mesh=mesh,
        in_specs=placed,
        out_specs=(P("shard"), P("clients", None), P()),
        check_vma=False,
    )
```

profile of v0, /device:TPU:0, one launch (start us, length us, event | category | flops | bytes accessed | tf_op | source)
XLA Modules:
  0.0 108.8 jit_solution(776859188835170135)
XLA Ops:
  0.6 1.4 %copy.7.seeds_ref = s32[64,1]{1,0:T(8,128)} copy(s32[64,1]{0,1:T(1,128)} %bitcast.15) | data formatting | bytes 512 | tf_op jit(solution)/shard_map/broadcast_in_dim | solution.py:398
  2.6 101.3 %aggregate_and_project.1 = (s32[4096,128]{1,0:T(8,128)}, s32[8,128]{1,0:T(8,128)}, s32[8,128]{1,0:T(8,128)}) custom-call(s32[1]{0:T(128)S(6)} %copy.9.alive_ref, s32[64,1]{1,0:T(8,128)} %copy.7.seeds_ref, s32[4096,128]{1,0:T(8,128)} %bitcast.12, s32[4096,128]{1,0:T(8,128)} %bitcast.13), custom_call_target="tpu_custom_call" | custom-call | tf_op jit(solution)/shard_map/aggregate_and_project/pallas_call | solution.py:365
  103.9 0.8 compare_select_fusion
  104.7 0.5 compare_select_fusion.2
  105.3 0.5 compare_select_fusion.4
  105.8 3.0 %copy.10 = s32[524288]{0:T(1024)} copy(s32[524288]{0:T(1024)} %bitcast.14) | data formatting | bytes 4194304
where the time goes:
time: 109 us
  Pallas kernels  101 us (93%)
  local copies, waits for them, and re-layouts  4.4 us (4%)
  other arithmetic  1.89 us (2%)
  between operations  1.29 us (1%)
    pallas_call x1, Pallas kernels, aggregate_and_project(): pl.pallas_call(functools.partial(aggregate_kernel, clients, length), in_s...  101 us
    unnamed x1, local copies, waits for them, and re-layouts  3.04 us

commit v1 on v0

v1 whole, which is shorter than its diff:
```python
import functools

import jax
import jax.numpy as jnp
from jax import lax
from jax.experimental import pallas as pl
from jax.experimental.pallas import tpu as pltpu
from jax.sharding import PartitionSpec as P

modulus = 2097143
mask21 = 2097151
LANES = 128
STREAMS = 4
AHEAD = 3
STRIDE = (LANES * 747796405 + 2147483648) % 4294967296 - 2147483648


def reduce_mod(x):
    x = (x & mask21) + (x >> 21) * 9
    return jnp.where(x >= modulus, x - modulus, x)


def wrap_once(x):
    return jnp.where(x >= modulus, x - modulus, x)


def packed_rows(count):
    tiles = count // 8
    return 8 * (2 * (tiles // 3) + tiles % 3)


def pack3(a, b, c):
    return a | (c << 21), b | ((c >> 11) << 21)


def unpack3(x, y):
    c = lax.shift_right_logical(x, 21) | ((y >> 21) << 11)
    return x & mask21, y & mask21, c


def each_step(tiles, fn):
    step = max(d for d in range(1, 9) if tiles % d == 0)

    def one(i):
        fn(i * step * 8, step * 8)

    if tiles == step:
        one(0)
    else:
        pl.loop(0, tiles // step)(one)


def pack_block(src, start, dst, at, count):
    third = 8 * (count // 24)
    rest = count - 3 * third

    def rows(x):
        return pl.multiple_of(x, 8)

    if third:

        def one(i, n):
            a = src[pl.ds(rows(start + i), n), :]
            b = src[pl.ds(rows(start + third + i), n), :]
            c = src[pl.ds(rows(start + 2 * third + i), n), :]
            x, y = pack3(a, b, c)
            dst[pl.ds(rows(at + i), n), :] = x
            dst[pl.ds(rows(at + third + i), n), :] = y

        each_step(third // 8, one)
    if rest:
        dst[pl.ds(rows(at + 2 * third), rest), :] = src[pl.ds(rows(start + 3 * third), rest), :]


def unpack_block(src, at, count, put):
    third = 8 * (count // 24)
    rest = count - 3 * third

    def rows(x):
        return pl.multiple_of(x, 8)

    if third:

        def one(i, n):
            x = src[pl.ds(rows(at + i), n), :]
            y = src[pl.ds(rows(at + third + i), n), :]
            for j, v in enumerate(unpack3(x, y)):
                put(j * third + i, n, v)

        each_step(third // 8, one)
    if rest:
        put(3 * third, rest, src[pl.ds(rows(at + 2 * third), rest), :])


def table_tile(start):
    v = start & 2147483647
    v = v ^ (v >> 15)
    v = (v * 277803737) & 2147483647
    v = v ^ (v >> 13)
    v = v * 1103515245
    v = v ^ (v >> 16)
    high = (v >> 5).astype(jnp.int8) & jnp.int8(31)
    low = v.astype(jnp.int8) & jnp.int8(31)
    return high.astype(jnp.bfloat16), low.astype(jnp.bfloat16)


def aggregate_kernel(
    clients,
    length,
    alive_ref,
    seeds_ref,
    quant_hbm,
    masks_hbm,
    agg_out,
    own_out,
    diff_out,
    quant,
    masked,
    base,
    partner,
    swap_from,
    swap_to,
    sent,
    arrived,
    gathered,
    own_parts,
    diff_parts,
    load_sem,
    swap_send,
    swap_recv,
    rs_send,
    rs_recv,
    ag_send,
    ag_recv,
    out_sem,
    own_send,
    own_recv,
    diff_send,
    diff_recv,
):
    rows = quant.shape[0]
    checks = seeds_ref.shape[0]
    bits = clients.bit_length() - 1
    me = lax.axis_index("clients")
    shards = lax.axis_size("shard")
    here = lax.axis_index("shard")
    start = here * length
    alive = alive_ref[0]
    stream = rows // STREAMS
    block = stream // clients
    unit = min(64, block)
    group = min(32, unit)
    per_block = block // unit
    others = clients // 2 - 1
    blocks = STREAMS * (others + 1)
    swap_rows = packed_rows(block)
    counts = [stream >> (i + 1) for i in range(bits)]
    sizes = [packed_rows(c) for c in counts]
    offsets = [sum(sizes[:i]) for i in range(bits)]
    per_stream = sum(sizes)

    barrier = pltpu.get_barrier_semaphore()
    for n in range(1, clients):
        pl.semaphore_signal(barrier, inc=1, device_id={"clients": me ^ n})
    for n in range(1, shards):
        there = lax.rem(here + n, shards)
        pl.semaphore_signal(barrier, inc=1, device_id={"shard": there})
        pl.semaphore_signal(barrier, inc=1, device_id={"shard": there, "clients": me ^ 1})
    peers = clients + 2 * shards - 3

    loads = []
    for h in range(STREAMS):
        at = pl.ds(h * stream, stream)
        loads.append(
            (
                pltpu.make_async_copy(quant_hbm.at[at], quant.at[at], load_sem.at[0, h]),
                pltpu.make_async_copy(masks_hbm.at[at], masked.at[at], load_sem.at[1, h]),
            )
        )
    for pair in loads:
        for copy in pair:
            copy.start()

    bit = [(me >> b) & 1 for b in range(bits)]
    share_even = sum(bit[i] << (bits - 1 - i) for i in range(bits))
    share_odd = sum(bit[(i + 1) % bits] << (bits - 1 - i) for i in range(bits))

    def share_of(h):
        return jnp.where(h % 2 == 1, share_odd, share_even)

    def partner_at(h, i):
        return me ^ jnp.where(h % 2 == 1, 1 << ((i + 1) % bits), 1 << i)

    def keep_row(h, i, flip=0):
        s = ((share_of(h) >> (bits - 1 - i)) ^ flip) << (bits - 1 - i)
        return pl.multiple_of(h * stream + s * block, 8)

    def block_row(w, flip=False):
        shared = w >= STREAMS * others
        h = w % STREAMS
        k = jnp.where(shared, 0, others - w // STREAMS)
        odd = h % 2 == 1
        k = jnp.where(odd, 2 * k, k)
        s = share_of(h) ^ k
        if flip:
            s = s ^ jnp.where(odd, 1, clients // 2)
        return pl.multiple_of(h * stream + s * block, 8)

    def swap_copy(w):
        at = pl.ds(pl.multiple_of(w * swap_rows, 8), swap_rows)
        return pltpu.make_async_remote_copy(
            src_ref=swap_from.at[at],
            dst_ref=swap_to.at[at],
            send_sem=swap_send.at[w],
            recv_sem=swap_recv.at[w],
            device_id={"clients": me ^ 1},
        )

    def rs_at(h, i):
        return pl.multiple_of(h * per_stream + offsets[i], 8)

    def rs_copy(h, i):
        at = pl.ds(rs_at(h, i), sizes[i])
        return pltpu.make_async_remote_copy(
            src_ref=sent.at[at],
            dst_ref=arrived.at[at],
            send_sem=rs_send.at[h, i],
            recv_sem=rs_recv.at[h, i],
            device_id={"clients": partner_at(h, i)},
        )

    def rs_pack(h, i):
        pack_block(masked, keep_row(h, i, 1), sent, rs_at(h, i), counts[i])

    def rs_take(h, i):
        rs_copy(h, i).wait()
        keep = keep_row(h, i)

        def put(at, n, v):
            spot = pl.ds(pl.multiple_of(keep + at, 8), n)
            masked[spot, :] = wrap_once(masked[spot, :] + v)

        unpack_block(arrived, rs_at(h, i), counts[i], put)

    def ag_slice(h, j, flip):
        s = ((share_of(h) >> j) ^ flip) << j
        at = pl.multiple_of((h * clients + s) * swap_rows, 8)
        return gathered.at[pl.ds(at, swap_rows << j)]

    def ag_copy(h, j, flip=0):
        return pltpu.make_async_remote_copy(
            src_ref=ag_slice(h, j, flip),
            dst_ref=ag_slice(h, j, flip),
            send_sem=ag_send.at[h, j],
            recv_sem=ag_recv.at[h, j],
            device_id={"clients": partner_at(h, bits - 1 - j)},
        )

    def store_copy(h):
        at = pl.ds(pl.multiple_of(h * clients * swap_rows, 8), clients * swap_rows)
        return pltpu.make_async_copy(gathered.at[at], agg_out.at[at], out_sem.at[h])

    lane = lax.broadcasted_iota(jnp.int32, (8, LANES), 1)
    sub = lax.broadcasted_iota(jnp.int32, (8, LANES), 0)
    lane = (lane + start) * 747796405
    for g in range(checks // 8):
        tile = lane
        for r in range(8):
            tile = tile + jnp.where(sub == r, seeds_ref[8 * g + r], 0)
        base[pl.ds(8 * g, 8), :] = tile

    step = min(64, stream)
    for h, pair in enumerate(loads):
        for copy in pair:
            copy.wait()

        @pl.loop(0, stream // step)
        def _(i, h=h):
            at = pl.ds(pl.multiple_of(h * stream + i * step, 8), step)
            s = wrap_once(wrap_once(quant[at, :] + masked[at, :]))
            masked[at, :] = s * alive

        rs_pack(h, 0)

    @pl.loop(0, blocks)
    def _(w):
        pack_block(quant, block_row(w, True), swap_from, w * swap_rows, block)

    pl.semaphore_wait(barrier, peers)
    swap_copy(0).start()
    for h in range(STREAMS):
        rs_copy(h, 0).start()
        if h == 0:
            for w in range(1, AHEAD):
                swap_copy(w).start()

    empty = jnp.zeros((8, LANES), jnp.float32)
    shift = 7 * (sub & 3)
    second = sub >= 4

    def work(u, total, share):
        w = u // per_block

        @pl.when(u % per_block == 0)
        def _():
            swap_copy(w).wait()

            @pl.when(w + AHEAD < blocks)
            def _():
                swap_copy(w + AHEAD).start()

            def put(at, n, v):
                partner[pl.ds(pl.multiple_of(at, 8), n), :] = v

            unpack_block(swap_to, w * swap_rows, block, put)

        inner = (u % per_block) * unit
        row = block_row(w) + inner
        for g in range(unit // group):
            highs, lows, pieces = [], [], []
            for k in range(g * group, (g + 1) * group):
                at = row + k
                high, low = table_tile(base[...] + at * STRIDE)
                highs.append(high)
                lows.append(low)
                one = jnp.broadcast_to(quant[pl.ds(at, 1), :], (8, LANES))
                two = jnp.broadcast_to(partner[pl.ds(inner + k, 1), :], (8, LANES))
                both = ((jnp.where(second, two, one) >> shift) & 127).astype(jnp.float32)
                third = empty
                if share:
                    three = jnp.broadcast_to(masked[pl.ds(at, 1), :], (8, LANES))
                    third = jnp.where(second, 0, (three >> shift) & 127).astype(jnp.float32)
                pieces.append(jnp.concatenate([both, third], 0).astype(jnp.bfloat16))
            table = jnp.concatenate([jnp.concatenate(highs, 1), jnp.concatenate(lows, 1)], 0)
            part = lax.dot_general(
                jnp.concatenate(pieces, 1),
                table,
                (((1,), (1,)), ((), ())),
                preferred_element_type=jnp.float32,
            )
            total = reduce_mod(total + part.astype(jnp.int32))
        return total

    units = blocks * per_block
    plain = STREAMS * others * per_block
    actions = bits * STREAMS
    early = units // 2
    first = min(3, early)

    def rs_stop(a):
        return first + (early - first) * a // actions

    def ag_stop(a):
        return early + (units - early) * (a + 1) // actions

    def compute(lo, hi, total, kinds):
        if "plain" in kinds:
            total = lax.fori_loop(
                lo, jnp.minimum(hi, plain), lambda u, t: work(u, t, False), total
            )
        if "share" in kinds:
            total = lax.fori_loop(
                jnp.maximum(lo, plain), hi, lambda u, t: work(u, t, True), total
            )
        return total

    total = jnp.zeros((16, LANES), jnp.int32)
    for i in range(bits):

        def turn(h, total, i=i):
            a = i * STREAMS + h
            lo = jnp.where(a == 0, 0, rs_stop(a - 1))
            total = compute(lo, rs_stop(a), total, ("plain",))
            rs_take(h, i)
            if i < bits - 1:
                rs_pack(h, i + 1)
                rs_copy(h, i + 1).start()
            else:
                spot = pl.multiple_of((h * clients + share_of(h)) * swap_rows, 8)
                pack_block(masked, keep_row(h, i), gathered, spot, block)
                ag_copy(h, 0).start()
            return total

        total = lax.fori_loop(0, STREAMS, turn, total)
    for j in range(bits):
        kinds = []
        lo_static = rs_stop(actions - 1) if j == 0 else ag_stop(j * STREAMS - 1)
        hi_static = ag_stop((j + 1) * STREAMS - 1)
        if lo_static < plain:
            kinds.append("plain")
        if hi_static > plain:
            kinds.append("share")

        def turn(h, total, j=j, kinds=tuple(kinds)):
            a = j * STREAMS + h
            lo = jnp.where(a == 0, rs_stop(actions - 1), ag_stop(a - 1))
            total = compute(lo, ag_stop(a), total, kinds)
            ag_copy(h, j).wait_send()
            ag_copy(h, j, 1).wait_recv()
            if j < bits - 1:
                ag_copy(h, j + 1).start()
            else:
                store_copy(h).start()
            return total

        total = lax.fori_loop(0, STREAMS, turn, total)

    own_parts[0] = total
    own_copies = []
    for n in range(1, 2 * shards):
        where = {"shard": lax.rem(here + n % shards, shards)} if n % shards else {}
        if n >= shards:
            where["clients"] = me ^ 1
        own_copies.append(
            pltpu.make_async_remote_copy(
                src_ref=own_parts.at[0],
                dst_ref=own_parts.at[n],
                send_sem=own_send.at[n],
                recv_sem=own_recv.at[n],
                device_id=where,
            )
        )
    for copy in own_copies:
        copy.start()
    for copy in own_copies:
        copy.wait()
    mine, theirs = own_parts[0], own_parts[shards]
    for n in range(1, shards):
        mine = mine + own_parts[n]
        theirs = theirs + own_parts[shards + n]
    total = reduce_mod(mine[:8] + pltpu.roll(theirs[:8], 4, 0))
    own_out[...] = total
    diff = reduce_mod(mine[8:]) - total * alive
    diff = jnp.where(diff < 0, diff + modulus, diff)
    diff_parts[0] = diff
    diff_copies = [
        pltpu.make_async_remote_copy(
            src_ref=diff_parts.at[0],
            dst_ref=diff_parts.at[n],
            send_sem=diff_send.at[n],
            recv_sem=diff_recv.at[n],
            device_id={"clients": me ^ n},
        )
        for n in range(1, clients)
    ]
    for copy in diff_copies:
        copy.start()
    for copy in diff_copies:
        copy.wait()
    for n in range(1, clients):
        diff = diff + diff_parts[n]
    diff_out[...] = reduce_mod(diff)
    for h in range(STREAMS):
        store_copy(h).wait()


def aggregate_and_project(quantized, pair_masks, alive_flags, row_seeds, clients, shards):
    length = quantized.shape[1]
    rows = length // LANES
    checks = row_seeds.shape[0]
    bits = clients.bit_length() - 1
    block = rows // STREAMS // clients
    blocks = STREAMS * clients // 2
    swap_rows = packed_rows(block)
    half_rows = STREAMS * sum(packed_rows(rows // STREAMS >> (i + 1)) for i in range(bits))
    gather_rows = STREAMS * clients * swap_rows
    vmem = pl.BlockSpec(memory_space=pltpu.VMEM)
    smem = pl.BlockSpec(memory_space=pltpu.SMEM)
    hbm = pl.BlockSpec(memory_space=pl.ANY)
    dma = pltpu.SemaphoreType.DMA
    return pl.pallas_call(
        functools.partial(aggregate_kernel, clients, length),
        in_specs=[smem, smem, hbm, hbm],
        out_specs=[hbm, vmem, vmem],
        out_shape=[
            jax.ShapeDtypeStruct((gather_rows, LANES), jnp.int32),
            jax.ShapeDtypeStruct((8, 2 * checks), jnp.int32),
            jax.ShapeDtypeStruct((8, 2 * checks), jnp.int32),
        ],
        scratch_shapes=[
            pltpu.VMEM((rows, LANES), jnp.int32),
            pltpu.VMEM((rows, LANES), jnp.int32),
            pltpu.VMEM((checks, LANES), jnp.int32),
            pltpu.VMEM((block, LANES), jnp.int32),
            pltpu.VMEM((blocks * swap_rows, LANES), jnp.int32),
            pltpu.VMEM((blocks * swap_rows, LANES), jnp.int32),
            pltpu.VMEM((half_rows, LANES), jnp.int32),
            pltpu.VMEM((half_rows, LANES), jnp.int32),
            pltpu.VMEM((gather_rows, LANES), jnp.int32),
            pltpu.VMEM((2 * shards, 16, 2 * checks), jnp.int32),
            pltpu.VMEM((clients, 8, 2 * checks), jnp.int32),
            dma((2, STREAMS)),
            dma((blocks,)),
            dma((blocks,)),
            dma((STREAMS, bits)),
            dma((STREAMS, bits)),
            dma((STREAMS, bits)),
            dma((STREAMS, bits)),
            dma((STREAMS,)),
            dma((2 * shards,)),
            dma((2 * shards,)),
            dma((clients,)),
            dma((clients,)),
        ],
        compiler_params=pltpu.CompilerParams(collective_id=0, has_side_effects=True),
        name="aggregate_and_project",
    )(
        alive_flags,
        row_seeds,
        quantized.reshape(rows, LANES),
        pair_masks.reshape(rows, LANES),
    )


def checksum(parts):
    checks = parts.shape[1] // 2
    parts = reduce_mod(parts[:, :checks] * 32 + parts[:, checks:])
    return reduce_mod(reduce_mod(parts[2:3] * 128 + parts[1:2]) * 128 + parts[0:1])


def finish_kernel(clients, packed, own, diff, agg_out, own_out, diff_out):
    block = agg_out.shape[0] // clients
    swap_rows = packed_rows(block)
    for n in range(clients):

        def put(at, count, v, n=n):
            agg_out[pl.ds(pl.multiple_of(n * block + at, 8), count), :] = v

        unpack_block(packed, n * swap_rows, block, put)
    own_out[...] = checksum(own[...])
    diff_out[...] = checksum(diff[...])


def finish(packed, own, diff, rows, clients):
    checks = own.shape[1] // 2
    small = pl.BlockSpec((8, 2 * checks), lambda i: (0, 0))
    result = pl.BlockSpec((1, checks), lambda i: (0, 0))
    return pl.pallas_call(
        functools.partial(finish_kernel, clients),
        grid=(STREAMS,),
        in_specs=[
            pl.BlockSpec((packed.shape[0] // STREAMS, LANES), lambda i: (i, 0)),
            small,
            small,
        ],
        out_specs=[pl.BlockSpec((rows // STREAMS, LANES), lambda i: (i, 0)), result, result],
        out_shape=[
            jax.ShapeDtypeStruct((rows, LANES), jnp.int32),
            jax.ShapeDtypeStruct((1, checks), jnp.int32),
            jax.ShapeDtypeStruct((1, checks), jnp.int32),
        ],
        name="finish",
    )(packed, own, diff)


def body(quantized, pair_masks, alive_flags, row_seeds):
    length = quantized.shape[1]
    clients = lax.axis_size("clients")
    shards = lax.axis_size("shard")
    packed, own, diff = aggregate_and_project(
        quantized, pair_masks, alive_flags, row_seeds, clients, shards
    )
    aggregate, own, diff = finish(packed, own, diff, length // LANES, clients)
    return (aggregate.reshape(length), own, diff.reshape(-1))


def solution(mesh):
    placed = (P("clients", "shard"), P("clients", "shard"), P("clients"), P())
    return jax.shard_map(
        body,
        mesh=mesh,
        in_specs=placed,
        out_specs=(P("shard"), P("clients", None), P()),
        check_vma=False,
    )
```

time: 109 us -> 71 us (0.65)
  Pallas kernels: 101 us -> 69.5 us
  local copies, waits for them, and re-layouts: 4.4 us -> 0 us
  other arithmetic: 1.89 us -> 0 us
    pallas_call x1, Pallas kernels: 101 us -> 65.8 us  [aggregate_and_project(): pl.pallas_call(functools.partial(aggregate_kernel, clients, length), in_s...]
    pallas_call x0 -> x1, Pallas kernels: none -> 3.69 us  [finish(): pl.pallas_call(functools.partial(finish_kernel, clients), grid=(STREAMS,)...]
    unnamed x1 -> x0, local copies, waits for them, and re-layouts: 3.04 us -> none
    select_n x3 -> x0, other arithmetic: 1.89 us -> none  [reduce_mod(): return jnp.where(x >= modulus, x - modulus, x)]
    broadcast_in_dim x1 -> x0, local copies, waits for them, and re-layouts: 1.36 us -> none  [aggregate_and_project(): row_seeds[:, None]]
where the time goes in v1:
time: 71 us; the launch traced here: 70.8 us
  Pallas kernels  69.5 us (98%)
  between operations  1.28 us (2%)
    pallas_call x1, Pallas kernels, aggregate_and_project(): pl.pallas_call(functools.partial(aggregate_kernel, clients, length), in_s...  65.8 us
    pallas_call x1, Pallas kernels, finish(): pl.pallas_call(functools.partial(finish_kernel, clients), grid=(STREAMS,)...  3.69 us

profile of v1, /device:TPU:0, one launch (start us, length us, event | category | flops | bytes accessed | tf_op | source)
XLA Modules:
  0.0 70.8 jit_solution(16697812960721972192)
XLA Ops:
  1.3 65.8 %aggregate_and_project.1 = (s32[2816,128]{1,0:T(8,128)}, s32[8,128]{1,0:T(8,128)}, s32[8,128]{1,0:T(8,128)}) custom-call(s32[1]{0:T(128)S(6)} %copy.7.alive_ref, s32[64]{0:T(128)} %seeds_ref.1, s32[4096,128]{1,0:T(8,128)} %bitcast.4, s32[4096,128]{1,0:T(8,128)} %bitcast.5), custom_call_target="tpu_custom_call" | custom-call | tf_op jit(solution)/shard_map/aggregate_and_project/pallas_call | solution.py:471
  67.1 3.7 %finish.1 = (s32[4096,128]{1,0:T(8,128)}, s32[1,64]{1,0:T(1,128)}, s32[1,64]{1,0:T(1,128)}) custom-call(s32[2816,128]{1,0:T(8,128)} %get-tuple-element.9.packed, s32[8,128]{1,0:T(8,128)} %get-tuple-element.10.own, s32[8,128]{1,0:T(8,128)} %get-tuple-element.11.diff), custom_call_target="tpu_custom_call" | custom-call | tf_op jit(solution)/shard_map/finish/pallas_call | solution.py:538

commit v2 on v1

--- a/solution.py
+++ b/solution.py
@@ -111,7 +111,7 @@
     seeds_ref,
     quant_hbm,
     masks_hbm,
-    agg_out,
+    gathered,
     own_out,
     diff_out,
     quant,
@@ -122,9 +122,9 @@
     swap_to,
     sent,
     arrived,
-    gathered,
     own_parts,
     diff_parts,
+    flags,
     load_sem,
     swap_send,
     swap_recv,
@@ -132,7 +132,7 @@
     rs_recv,
     ag_send,
     ag_recv,
-    out_sem,
+    flag_sem,
     own_send,
     own_recv,
     diff_send,
@@ -160,13 +160,11 @@
     per_stream = sum(sizes)
 
     barrier = pltpu.get_barrier_semaphore()
-    for n in range(1, clients):
-        pl.semaphore_signal(barrier, inc=1, device_id={"clients": me ^ n})
+    for b in range(bits):
+        pl.semaphore_signal(barrier, inc=1, device_id={"clients": me ^ (1 << b)})
     for n in range(1, shards):
-        there = lax.rem(here + n, shards)
-        pl.semaphore_signal(barrier, inc=1, device_id={"shard": there})
-        pl.semaphore_signal(barrier, inc=1, device_id={"shard": there, "clients": me ^ 1})
-    peers = clients + 2 * shards - 3
+        pl.semaphore_signal(barrier, inc=1, device_id={"shard": lax.rem(here + n, shards)})
+    peers = bits + shards - 1
 
     loads = []
     for h in range(STREAMS):
@@ -256,10 +254,6 @@
             device_id={"clients": partner_at(h, bits - 1 - j)},
         )
 
-    def store_copy(h):
-        at = pl.ds(pl.multiple_of(h * clients * swap_rows, 8), clients * swap_rows)
-        return pltpu.make_async_copy(gathered.at[at], agg_out.at[at], out_sem.at[h])
-
     lane = lax.broadcasted_iota(jnp.int32, (8, LANES), 1)
     sub = lax.broadcasted_iota(jnp.int32, (8, LANES), 0)
     lane = (lane + start) * 747796405
@@ -286,8 +280,18 @@
     def _(w):
         pack_block(quant, block_row(w, True), swap_from, w * swap_rows, block)
 
+    flags[0] = jnp.full((8, LANES), alive)
+    flag_copy = pltpu.make_async_remote_copy(
+        src_ref=flags.at[0],
+        dst_ref=flags.at[1],
+        send_sem=flag_sem.at[0],
+        recv_sem=flag_sem.at[1],
+        device_id={"clients": me ^ 1},
+    )
+
     pl.semaphore_wait(barrier, peers)
     swap_copy(0).start()
+    flag_copy.start()
     for h in range(STREAMS):
         rs_copy(h, 0).start()
         if h == 0:
@@ -399,59 +403,55 @@
             ag_copy(h, j, 1).wait_recv()
             if j < bits - 1:
                 ag_copy(h, j + 1).start()
-            else:
-                store_copy(h).start()
             return total
 
         total = lax.fori_loop(0, STREAMS, turn, total)
 
-    own_parts[0] = total
-    own_copies = []
+    flag_copy.wait()
+    own = total[:8]
+    diff = total[8:] - own * alive - pltpu.roll(own, 4, 0) * flags[1]
+    diff = jnp.where(diff < 0, diff + modulus, diff)
+    diff = jnp.where(diff < 0, diff + modulus, diff)
+    own_parts[0] = own
+    diff_parts[0] = diff
+
+    def own_copy(n):
+        return pltpu.make_async_remote_copy(
+            src_ref=own_parts.at[0],
+            dst_ref=own_parts.at[n],
+            send_sem=own_send.at[n],
+            recv_sem=own_recv.at[n],
+            device_id={"clients": me ^ (n // shards), "shard": (here + n) % shards},
+        )
+
+    def diff_copy(n):
+        return pltpu.make_async_remote_copy(
+            src_ref=diff_parts.at[0],
+            dst_ref=diff_parts.at[n],
+            send_sem=diff_send.at[n],
+            recv_sem=diff_recv.at[n],
+            device_id={"clients": me ^ (n // shards), "shard": (here + n) % shards},
+        )
+
+    @pl.loop(1, clients * shards)
+    def _(n):
+        diff_copy(clients * shards - n).start()
+
     for n in range(1, 2 * shards):
-        where = {"shard": lax.rem(here + n % shards, shards)} if n % shards else {}
-        if n >= shards:
-            where["clients"] = me ^ 1
-        own_copies.append(
-            pltpu.make_async_remote_copy(
-                src_ref=own_parts.at[0],
-                dst_ref=own_parts.at[n],
-                send_sem=own_send.at[n],
-                recv_sem=own_recv.at[n],
-                device_id=where,
-            )
-        )
-    for copy in own_copies:
-        copy.start()
-    for copy in own_copies:
-        copy.wait()
+        own_copy(n).start()
+    for n in range(1, 2 * shards):
+        own_copy(n).wait()
     mine, theirs = own_parts[0], own_parts[shards]
     for n in range(1, shards):
         mine = mine + own_parts[n]
         theirs = theirs + own_parts[shards + n]
-    total = reduce_mod(mine[:8] + pltpu.roll(theirs[:8], 4, 0))
-    own_out[...] = total
-    diff = reduce_mod(mine[8:]) - total * alive
-    diff = jnp.where(diff < 0, diff + modulus, diff)
-    diff_parts[0] = diff
-    diff_copies = [
-        pltpu.make_async_remote_copy(
-            src_ref=diff_parts.at[0],
-            dst_ref=diff_parts.at[n],
-            send_sem=diff_send.at[n],
-            recv_sem=diff_recv.at[n],
-            device_id={"clients": me ^ n},
-        )
-        for n in range(1, clients)
-    ]
-    for copy in diff_copies:
-        copy.start()
-    for copy in diff_copies:
-        copy.wait()
-    for n in range(1, clients):
-        diff = diff + diff_parts[n]
-    diff_out[...] = reduce_mod(diff)
-    for h in range(STREAMS):
-        store_copy(h).wait()
+    own_out[...] = reduce_mod(mine + pltpu.roll(theirs, 4, 0))
+
+    def add_diff(n, diff):
+        diff_copy(n).wait()
+        return diff + diff_parts[n]
+
+    diff_out[...] = reduce_mod(lax.fori_loop(1, clients * shards, add_diff, diff))
 
 
 def aggregate_and_project(quantized, pair_masks, alive_flags, row_seeds, clients, shards):
@@ -471,11 +471,11 @@
     return pl.pallas_call(
         functools.partial(aggregate_kernel, clients, length),
         in_specs=[smem, smem, hbm, hbm],
-        out_specs=[hbm, vmem, vmem],
+        out_specs=[vmem, vmem, vmem],
         out_shape=[
-            jax.ShapeDtypeStruct((gather_rows, LANES), jnp.int32),
-            jax.ShapeDtypeStruct((8, 2 * checks), jnp.int32),
-            jax.ShapeDtypeStruct((8, 2 * checks), jnp.int32),
+            pltpu.VMEM((gather_rows, LANES), jnp.int32),
+            pltpu.VMEM((8, 2 * checks), jnp.int32),
+            pltpu.VMEM((8, 2 * checks), jnp.int32),
         ],
         scratch_shapes=[
             pltpu.VMEM((rows, LANES), jnp.int32),
@@ -486,9 +486,9 @@
             pltpu.VMEM((blocks * swap_rows, LANES), jnp.int32),
             pltpu.VMEM((half_rows, LANES), jnp.int32),
             pltpu.VMEM((half_rows, LANES), jnp.int32),
-            pltpu.VMEM((gather_rows, LANES), jnp.int32),
-            pltpu.VMEM((2 * shards, 16, 2 * checks), jnp.int32),
-            pltpu.VMEM((clients, 8, 2 * checks), jnp.int32),
+            pltpu.VMEM((2 * shards, 8, 2 * checks), jnp.int32),
+            pltpu.VMEM((clients * shards, 8, 2 * checks), jnp.int32),
+            pltpu.VMEM((2, 8, LANES), jnp.int32),
             dma((2, STREAMS)),
             dma((blocks,)),
             dma((blocks,)),
@@ -496,11 +496,11 @@
             dma((STREAMS, bits)),
             dma((STREAMS, bits)),
             dma((STREAMS, bits)),
-            dma((STREAMS,)),
+            dma((2,)),
             dma((2 * shards,)),
             dma((2 * shards,)),
-            dma((clients,)),
-            dma((clients,)),
+            dma((clients * shards,)),
+            dma((clients * shards,)),
         ],
         compiler_params=pltpu.CompilerParams(collective_id=0, has_side_effects=True),
         name="aggregate_and_project",
@@ -521,34 +521,33 @@
 def finish_kernel(clients, packed, own, diff, agg_out, own_out, diff_out):
     block = agg_out.shape[0] // clients
     swap_rows = packed_rows(block)
-    for n in range(clients):
-
-        def put(at, count, v, n=n):
+    first = pl.program_id(0) * clients
+
+    @pl.loop(0, clients)
+    def _(n):
+        def put(at, count, v):
             agg_out[pl.ds(pl.multiple_of(n * block + at, 8), count), :] = v
 
-        unpack_block(packed, n * swap_rows, block, put)
+        unpack_block(packed, (first + n) * swap_rows, block, put)
+
     own_out[...] = checksum(own[...])
     diff_out[...] = checksum(diff[...])
 
 
 def finish(packed, own, diff, rows, clients):
     checks = own.shape[1] // 2
-    small = pl.BlockSpec((8, 2 * checks), lambda i: (0, 0))
-    result = pl.BlockSpec((1, checks), lambda i: (0, 0))
+    vmem = pl.BlockSpec(memory_space=pltpu.VMEM)
     return pl.pallas_call(
         functools.partial(finish_kernel, clients),
         grid=(STREAMS,),
-        in_specs=[
-            pl.BlockSpec((packed.shape[0] // STREAMS, LANES), lambda i: (i, 0)),
-            small,
-            small,
-        ],
-        out_specs=[pl.BlockSpec((rows // STREAMS, LANES), lambda i: (i, 0)), result, result],
+        in_specs=[vmem, vmem, vmem],
+        out_specs=[pl.BlockSpec((rows // STREAMS, LANES), lambda i: (i, 0)), vmem, vmem],
         out_shape=[
             jax.ShapeDtypeStruct((rows, LANES), jnp.int32),
             jax.ShapeDtypeStruct((1, checks), jnp.int32),
             jax.ShapeDtypeStruct((1, checks), jnp.int32),
         ],
+        compiler_params=pltpu.CompilerParams(vmem_limit_bytes=16 * 1024 * 1024),
         name="finish",
     )(packed, own, diff)
 

time: 71 us -> 66.3 us (0.934)
  Pallas kernels: 69.5 us -> 64.8 us
    pallas_call x1, Pallas kernels: 65.8 us -> 62.9 us  [aggregate_and_project(): pl.pallas_call(functools.partial(aggregate_kernel, clients, length), in_s...]
    pallas_call x1, Pallas kernels: 3.69 us -> 1.95 us  [finish(): pl.pallas_call(functools.partial(finish_kernel, clients), grid=(STREAMS,)...]
where the time goes in v2:
time: 66.3 us; the launch traced here: 66.1 us
  Pallas kernels  64.8 us (98%)
  between operations  1.28 us (2%)
    pallas_call x1, Pallas kernels, aggregate_and_project(): pl.pallas_call(functools.partial(aggregate_kernel, clients, length), in_s...  62.9 us
    pallas_call x1, Pallas kernels, finish(): pl.pallas_call(functools.partial(finish_kernel, clients), grid=(STREAMS,)...  1.95 us

profile of v2, /device:TPU:0, one launch (start us, length us, event | category | flops | bytes accessed | tf_op | source)
XLA Modules:
  0.0 66.1 jit_solution(11953121084469256656)
XLA Ops:
  1.3 62.9 %aggregate_and_project.1 = (s32[2816,128]{1,0:T(8,128)S(1)}, s32[8,128]{1,0:T(8,128)S(1)}, s32[8,128]{1,0:T(8,128)S(1)}) custom-call(s32[1]{0:T(128)S(6)} %copy.7.alive_ref, s32[64]{0:T(128)} %seeds_ref.1, s32[4096,128]{1,0:T(8,128)} %bitcast.4, s32[4096,128]{1,0:T(8,128)} %bitcast.5), custom_call_target="tpu_custom_call" | custom-call | tf_op jit(solution)/shard_map/aggregate_and_project/pallas_call | solution.py:471
  64.2 2.0 %finish.1 = (s32[4096,128]{1,0:T(8,128)}, s32[1,64]{1,0:T(1,128)}, s32[1,64]{1,0:T(1,128)}) custom-call(s32[2816,128]{1,0:T(8,128)S(1)} %get-tuple-element.9.packed, s32[8,128]{1,0:T(8,128)S(1)} %get-tuple-element.10.own, s32[8,128]{1,0:T(8,128)S(1)} %get-tuple-element.11.diff), custom_call_target="tpu_custom_call" | custom-call | tf_op jit(solution)/shard_map/finish/pallas_call | solution.py:540

commit v3 on v2

--- a/solution.py
+++ b/solution.py
@@ -112,8 +112,7 @@
     quant_hbm,
     masks_hbm,
     gathered,
-    own_out,
-    diff_out,
+    sums_out,
     quant,
     masked,
     base,
@@ -122,8 +121,8 @@
     swap_to,
     sent,
     arrived,
-    own_parts,
-    diff_parts,
+    rows_out,
+    rows_in,
     flags,
     load_sem,
     swap_send,
@@ -133,13 +132,11 @@
     ag_send,
     ag_recv,
     flag_sem,
-    own_send,
-    own_recv,
-    diff_send,
-    diff_recv,
+    sums_sem,
 ):
     rows = quant.shape[0]
     checks = seeds_ref.shape[0]
+    devices = rows_in.shape[0]
     bits = clients.bit_length() - 1
     me = lax.axis_index("clients")
     shards = lax.axis_size("shard")
@@ -355,7 +352,7 @@
         return first + (early - first) * a // actions
 
     def ag_stop(a):
-        return early + (units - early) * (a + 1) // actions
+        return early + (units - early) * (a + 1) // (actions - STREAMS)
 
     def compute(lo, hi, total, kinds):
         if "plain" in kinds:
@@ -373,6 +370,7 @@
 
         def turn(h, total, i=i):
             a = i * STREAMS + h
+            h = h ^ 1
             lo = jnp.where(a == 0, 0, rs_stop(a - 1))
             total = compute(lo, rs_stop(a), total, ("plain",))
             rs_take(h, i)
@@ -386,7 +384,13 @@
             return total
 
         total = lax.fori_loop(0, STREAMS, turn, total)
-    for j in range(bits):
+    def gather_turn(h, j):
+        ag_copy(h, j).wait_send()
+        ag_copy(h, j, 1).wait_recv()
+        if j < bits - 1:
+            ag_copy(h, j + 1).start()
+
+    for j in range(bits - 1):
         kinds = []
         lo_static = rs_stop(actions - 1) if j == 0 else ag_stop(j * STREAMS - 1)
         hi_static = ag_stop((j + 1) * STREAMS - 1)
@@ -397,61 +401,56 @@
 
         def turn(h, total, j=j, kinds=tuple(kinds)):
             a = j * STREAMS + h
+            h = h ^ 1
             lo = jnp.where(a == 0, rs_stop(actions - 1), ag_stop(a - 1))
             total = compute(lo, ag_stop(a), total, kinds)
-            ag_copy(h, j).wait_send()
-            ag_copy(h, j, 1).wait_recv()
-            if j < bits - 1:
-                ag_copy(h, j + 1).start()
+            gather_turn(h, j)
             return total
 
         total = lax.fori_loop(0, STREAMS, turn, total)
 
     flag_copy.wait()
-    own = total[:8]
-    diff = total[8:] - own * alive - pltpu.roll(own, 4, 0) * flags[1]
+    total = reduce_mod(total * 32 + pltpu.roll(total, checks, 1))
+
+    def combine(r):
+        high = reduce_mod(total[r + 2 : r + 3] * 128 + total[r + 1 : r + 2])
+        return reduce_mod(high * 128 + total[r : r + 1])
+
+    own, other = combine(0), combine(4)
+    diff = combine(8) - own * alive - other * flags[1, :1]
     diff = jnp.where(diff < 0, diff + modulus, diff)
     diff = jnp.where(diff < 0, diff + modulus, diff)
-    own_parts[0] = own
-    diff_parts[0] = diff
-
-    def own_copy(n):
+    left = lax.broadcasted_iota(jnp.int32, (1, LANES), 1) < checks
+    mine = jnp.where(left, diff, pltpu.roll(own, checks, 1))
+    rows_out[0] = mine
+    rows_out[1] = jnp.where(left, diff, pltpu.roll(other, checks, 1))
+    rows_in[0] = mine
+
+    def row_copy(n):
         return pltpu.make_async_remote_copy(
-            src_ref=own_parts.at[0],
-            dst_ref=own_parts.at[n],
-            send_sem=own_send.at[n],
-            recv_sem=own_recv.at[n],
+            src_ref=rows_out.at[jnp.where(n // shards == 1, 1, 0)],
+            dst_ref=rows_in.at[n],
+            send_sem=sums_sem.at[0],
+            recv_sem=sums_sem.at[1],
             device_id={"clients": me ^ (n // shards), "shard": (here + n) % shards},
         )
 
-    def diff_copy(n):
-        return pltpu.make_async_remote_copy(
-            src_ref=diff_parts.at[0],
-            dst_ref=diff_parts.at[n],
-            send_sem=diff_send.at[n],
-            recv_sem=diff_recv.at[n],
-            device_id={"clients": me ^ (n // shards), "shard": (here + n) % shards},
-        )
-
-    @pl.loop(1, clients * shards)
+    @pl.loop(1, devices)
     def _(n):
-        diff_copy(clients * shards - n).start()
-
+        row_copy(devices - n).start()
+
+    @pl.loop(0, STREAMS)
+    def _(h):
+        gather_turn(h ^ 1, bits - 1)
+
+    landed = rows_in.at[pl.ds(1, devices - 1)]
+    pltpu.make_async_copy(landed, landed, sums_sem.at[0]).wait()
+    pltpu.make_async_copy(landed, landed, sums_sem.at[1]).wait()
+    near = rows_in[0]
     for n in range(1, 2 * shards):
-        own_copy(n).start()
-    for n in range(1, 2 * shards):
-        own_copy(n).wait()
-    mine, theirs = own_parts[0], own_parts[shards]
-    for n in range(1, shards):
-        mine = mine + own_parts[n]
-        theirs = theirs + own_parts[shards + n]
-    own_out[...] = reduce_mod(mine + pltpu.roll(theirs, 4, 0))
-
-    def add_diff(n, diff):
-        diff_copy(n).wait()
-        return diff + diff_parts[n]
-
-    diff_out[...] = reduce_mod(lax.fori_loop(1, clients * shards, add_diff, diff))
+        near = near + rows_in[n]
+    every = lax.fori_loop(2 * shards, devices, lambda n, t: t + rows_in[n], near)
+    sums_out[...] = reduce_mod(jnp.where(left, every, near))
 
 
 def aggregate_and_project(quantized, pair_masks, alive_flags, row_seeds, clients, shards):
@@ -471,11 +470,10 @@
     return pl.pallas_call(
         functools.partial(aggregate_kernel, clients, length),
         in_specs=[smem, smem, hbm, hbm],
-        out_specs=[vmem, vmem, vmem],
+        out_specs=[vmem, vmem],
         out_shape=[
             pltpu.VMEM((gather_rows, LANES), jnp.int32),
-            pltpu.VMEM((8, 2 * checks), jnp.int32),
-            pltpu.VMEM((8, 2 * checks), jnp.int32),
+            pltpu.VMEM((1, 2 * checks), jnp.int32),
         ],
         scratch_shapes=[
             pltpu.VMEM((rows, LANES), jnp.int32),
@@ -486,8 +484,8 @@
             pltpu.VMEM((blocks * swap_rows, LANES), jnp.int32),
             pltpu.VMEM((half_rows, LANES), jnp.int32),
             pltpu.VMEM((half_rows, LANES), jnp.int32),
-            pltpu.VMEM((2 * shards, 8, 2 * checks), jnp.int32),
-            pltpu.VMEM((clients * shards, 8, 2 * checks), jnp.int32),
+            pltpu.VMEM((2, 1, 2 * checks), jnp.int32),
+            pltpu.VMEM((clients * shards, 1, 2 * checks), jnp.int32),
             pltpu.VMEM((2, 8, LANES), jnp.int32),
             dma((2, STREAMS)),
             dma((blocks,)),
@@ -497,10 +495,7 @@
             dma((STREAMS, bits)),
             dma((STREAMS, bits)),
             dma((2,)),
-            dma((2 * shards,)),
-            dma((2 * shards,)),
-            dma((clients * shards,)),
-            dma((clients * shards,)),
+            dma((2,)),
         ],
         compiler_params=pltpu.CompilerParams(collective_id=0, has_side_effects=True),
         name="aggregate_and_project",
@@ -512,13 +507,7 @@
     )
 
 
-def checksum(parts):
-    checks = parts.shape[1] // 2
-    parts = reduce_mod(parts[:, :checks] * 32 + parts[:, checks:])
-    return reduce_mod(reduce_mod(parts[2:3] * 128 + parts[1:2]) * 128 + parts[0:1])
-
-
-def finish_kernel(clients, packed, own, diff, agg_out, own_out, diff_out):
+def finish_kernel(clients, packed, sums, agg_out, own_out, diff_out):
     block = agg_out.shape[0] // clients
     swap_rows = packed_rows(block)
     first = pl.program_id(0) * clients
@@ -530,17 +519,18 @@
 
         unpack_block(packed, (first + n) * swap_rows, block, put)
 
-    own_out[...] = checksum(own[...])
-    diff_out[...] = checksum(diff[...])
-
-
-def finish(packed, own, diff, rows, clients):
-    checks = own.shape[1] // 2
+    checks = own_out.shape[1]
+    diff_out[...] = sums[:, :checks]
+    own_out[...] = sums[:, checks:]
+
+
+def finish(packed, sums, rows, clients):
+    checks = sums.shape[1] // 2
     vmem = pl.BlockSpec(memory_space=pltpu.VMEM)
     return pl.pallas_call(
         functools.partial(finish_kernel, clients),
         grid=(STREAMS,),
-        in_specs=[vmem, vmem, vmem],
+        in_specs=[vmem, vmem],
         out_specs=[pl.BlockSpec((rows // STREAMS, LANES), lambda i: (i, 0)), vmem, vmem],
         out_shape=[
             jax.ShapeDtypeStruct((rows, LANES), jnp.int32),
@@ -549,17 +539,17 @@
         ],
         compiler_params=pltpu.CompilerParams(vmem_limit_bytes=16 * 1024 * 1024),
         name="finish",
-    )(packed, own, diff)
+    )(packed, sums)
 
 
 def body(quantized, pair_masks, alive_flags, row_seeds):
     length = quantized.shape[1]
     clients = lax.axis_size("clients")
     shards = lax.axis_size("shard")
-    packed, own, diff = aggregate_and_project(
+    packed, sums = aggregate_and_project(
         quantized, pair_masks, alive_flags, row_seeds, clients, shards
     )
-    aggregate, own, diff = finish(packed, own, diff, length // LANES, clients)
+    aggregate, own, diff = finish(packed, sums, length // LANES, clients)
     return (aggregate.reshape(length), own, diff.reshape(-1))
 
 

time: 66.3 us -> 64.2 us (0.968)
  Pallas kernels: 64.8 us -> 62.8 us
    pallas_call x1, Pallas kernels: 62.9 us -> 60.8 us  [aggregate_and_project(): pl.pallas_call(functools.partial(aggregate_kernel, clients, length), in_s...]
where the time goes in v3:
time: 64.2 us; the launch traced here: 64.1 us
  Pallas kernels  62.8 us (98%)
  between operations  1.29 us (2%)
    pallas_call x1, Pallas kernels, aggregate_and_project(): pl.pallas_call(functools.partial(aggregate_kernel, clients, length), in_s...  60.8 us
    pallas_call x1, Pallas kernels, finish(): pl.pallas_call(functools.partial(finish_kernel, clients), grid=(STREAMS,)...  1.94 us

profile of v3, /device:TPU:0, one launch (start us, length us, event | category | flops | bytes accessed | tf_op | source)
XLA Modules:
  0.0 64.1 jit_solution(14160522023957531959)
XLA Ops:
  1.3 60.8 %aggregate_and_project.1 = (s32[2816,128]{1,0:T(8,128)S(1)}, s32[1,128]{1,0:T(1,128)S(1)}) custom-call(s32[1]{0:T(128)S(6)} %copy.7.alive_ref, s32[64]{0:T(128)} %seeds_ref.1, s32[4096,128]{1,0:T(8,128)} %bitcast.4, s32[4096,128]{1,0:T(8,128)} %bitcast.5), custom_call_target="tpu_custom_call" | custom-call | tf_op jit(solution)/shard_map/aggregate_and_project/pallas_call | solution.py:470
  62.1 1.9 %finish.1 = (s32[4096,128]{1,0:T(8,128)}, s32[1,64]{1,0:T(1,128)}, s32[1,64]{1,0:T(1,128)}) custom-call(s32[2816,128]{1,0:T(8,128)S(1)} %get-tuple-element.8.packed, s32[1,128]{1,0:T(1,128)S(1)} %get-tuple-element.9.sums), custom_call_target="tpu_custom_call" | custom-call | tf_op jit(solution)/shard_map/finish/pallas_call | solution.py:530

commit v4 on v3

--- a/solution.py
+++ b/solution.py
@@ -145,7 +145,7 @@
     alive = alive_ref[0]
     stream = rows // STREAMS
     block = stream // clients
-    unit = min(64, block)
+    unit = min(128, block)
     group = min(32, unit)
     per_block = block // unit
     others = clients // 2 - 1
@@ -163,6 +163,7 @@
         pl.semaphore_signal(barrier, inc=1, device_id={"shard": lax.rem(here + n, shards)})
     peers = bits + shards - 1
 
+    order = [h ^ 1 for h in range(STREAMS)]
     loads = []
     for h in range(STREAMS):
         at = pl.ds(h * stream, stream)
@@ -172,9 +173,9 @@
                 pltpu.make_async_copy(masks_hbm.at[at], masked.at[at], load_sem.at[1, h]),
             )
         )
-    for pair in loads:
-        for copy in pair:
-            copy.start()
+    for side in range(2):
+        for h in order:
+            loads[h][side].start()
 
     bit = [(me >> b) & 1 for b in range(bits)]
     share_even = sum(bit[i] << (bits - 1 - i) for i in range(bits))
@@ -260,21 +261,7 @@
             tile = tile + jnp.where(sub == r, seeds_ref[8 * g + r], 0)
         base[pl.ds(8 * g, 8), :] = tile
 
-    step = min(64, stream)
-    for h, pair in enumerate(loads):
-        for copy in pair:
-            copy.wait()
-
-        @pl.loop(0, stream // step)
-        def _(i, h=h):
-            at = pl.ds(pl.multiple_of(h * stream + i * step, 8), step)
-            s = wrap_once(wrap_once(quant[at, :] + masked[at, :]))
-            masked[at, :] = s * alive
-
-        rs_pack(h, 0)
-
-    @pl.loop(0, blocks)
-    def _(w):
+    def swap_pack(w):
         pack_block(quant, block_row(w, True), swap_from, w * swap_rows, block)
 
     flags[0] = jnp.full((8, LANES), alive)
@@ -286,14 +273,28 @@
         device_id={"clients": me ^ 1},
     )
 
+    for h in order:
+        loads[h][0].wait()
+    pl.loop(0, AHEAD)(swap_pack)
     pl.semaphore_wait(barrier, peers)
     swap_copy(0).start()
-    flag_copy.start()
-    for h in range(STREAMS):
+    step = min(64, stream)
+    for n, h in enumerate(order):
+        loads[h][1].wait()
+
+        @pl.loop(0, stream // step)
+        def _(i, h=h):
+            at = pl.ds(pl.multiple_of(h * stream + i * step, 8), step)
+            s = wrap_once(wrap_once(quant[at, :] + masked[at, :]))
+            masked[at, :] = s * alive
+
+        rs_pack(h, 0)
         rs_copy(h, 0).start()
-        if h == 0:
+        if n == 1:
             for w in range(1, AHEAD):
                 swap_copy(w).start()
+    flag_copy.start()
+    pl.loop(AHEAD, blocks)(swap_pack)
 
     empty = jnp.zeros((8, LANES), jnp.float32)
     shift = 7 * (sub & 3)
@@ -345,8 +346,8 @@
     units = blocks * per_block
     plain = STREAMS * others * per_block
     actions = bits * STREAMS
-    early = units // 2
-    first = min(3, early)
+    early = units * 9 // 16
+    first = min(2, early)
 
     def rs_stop(a):
         return first + (early - first) * a // actions

time: 64.2 us -> 61.3 us (0.955)
  Pallas kernels: 62.8 us -> 59.8 us
    pallas_call x1, Pallas kernels: 60.8 us -> 57.9 us  [aggregate_and_project(): pl.pallas_call(functools.partial(aggregate_kernel, clients, length), in_s...]
where the time goes in v4:
time: 61.3 us; the launch traced here: 61.1 us
  Pallas kernels  59.8 us (98%)
  between operations  1.29 us (2%)
    pallas_call x1, Pallas kernels, aggregate_and_project(): pl.pallas_call(functools.partial(aggregate_kernel, clients, length), in_s...  57.9 us
    pallas_call x1, Pallas kernels, finish(): pl.pallas_call(functools.partial(finish_kernel, clients), grid=(STREAMS,)...  1.94 us

profile of v4, /device:TPU:0, one launch (start us, length us, event | category | flops | bytes accessed | tf_op | source)
XLA Modules:
  0.0 61.1 jit_solution(6453692060187717005)
XLA Ops:
  1.3 57.9 %aggregate_and_project.1 = (s32[2816,128]{1,0:T(8,128)S(1)}, s32[1,128]{1,0:T(1,128)S(1)}) custom-call(s32[1]{0:T(128)S(6)} %copy.7.alive_ref, s32[64]{0:T(128)} %seeds_ref.1, s32[4096,128]{1,0:T(8,128)} %bitcast.4, s32[4096,128]{1,0:T(8,128)} %bitcast.5), custom_call_target="tpu_custom_call" | custom-call | tf_op jit(solution)/shard_map/aggregate_and_project/pallas_call | solution.py:471
  59.2 1.9 %finish.1 = (s32[4096,128]{1,0:T(8,128)}, s32[1,64]{1,0:T(1,128)}, s32[1,64]{1,0:T(1,128)}) custom-call(s32[2816,128]{1,0:T(8,128)S(1)} %get-tuple-element.8.packed, s32[1,128]{1,0:T(1,128)S(1)} %get-tuple-element.9.sums), custom_call_target="tpu_custom_call" | custom-call | tf_op jit(solution)/shard_map/finish/pallas_call | solution.py:531

commit v5 on v4

--- a/solution.py
+++ b/solution.py
@@ -146,7 +146,7 @@
     stream = rows // STREAMS
     block = stream // clients
     unit = min(128, block)
-    group = min(32, unit)
+    group = min(64, unit)
     per_block = block // unit
     others = clients // 2 - 1
     blocks = STREAMS * (others + 1)
@@ -254,12 +254,12 @@
 
     lane = lax.broadcasted_iota(jnp.int32, (8, LANES), 1)
     sub = lax.broadcasted_iota(jnp.int32, (8, LANES), 0)
-    lane = (lane + start) * 747796405
-    for g in range(checks // 8):
-        tile = lane
-        for r in range(8):
-            tile = tile + jnp.where(sub == r, seeds_ref[8 * g + r], 0)
-        base[pl.ds(8 * g, 8), :] = tile
+    seeds = jnp.zeros((8, LANES), jnp.int32)
+    for r in range(checks):
+        seeds = jnp.where(lane % checks == r, seeds_ref[r], seeds)
+    for g in range(LANES // 8):
+        spot = start + 8 * g + sub + lane // checks * LANES
+        base[pl.ds(8 * g, 8), :] = spot * 747796405 + seeds
 
     def swap_pack(w):
         pack_block(quant, block_row(w, True), swap_from, w * swap_rows, block)
@@ -300,6 +300,11 @@
     shift = 7 * (sub & 3)
     second = sub >= 4
 
+    def split(first_ref, a, second_ref, b):
+        one = jnp.broadcast_to(first_ref[pl.ds(a, 1), :], (8, LANES))
+        two = jnp.broadcast_to(second_ref[pl.ds(b, 1), :], (8, LANES))
+        return ((jnp.where(second, two, one) >> shift) & 127).astype(jnp.float32)
+
     def work(u, total, share):
         w = u // per_block
 
@@ -319,28 +324,26 @@
         inner = (u % per_block) * unit
         row = block_row(w) + inner
         for g in range(unit // group):
-            highs, lows, pieces = [], [], []
-            for k in range(g * group, (g + 1) * group):
+            tables, pieces = [], []
+            for k in range(g * group, (g + 1) * group, 2):
                 at = row + k
                 high, low = table_tile(base[...] + at * STRIDE)
-                highs.append(high)
-                lows.append(low)
-                one = jnp.broadcast_to(quant[pl.ds(at, 1), :], (8, LANES))
-                two = jnp.broadcast_to(partner[pl.ds(inner + k, 1), :], (8, LANES))
-                both = ((jnp.where(second, two, one) >> shift) & 127).astype(jnp.float32)
-                third = empty
+                tables.append(jnp.concatenate([high, low], 1))
+                parts = [split(quant, at, partner, inner + k)]
+                parts.append(split(quant, at + 1, partner, inner + k + 1))
                 if share:
-                    three = jnp.broadcast_to(masked[pl.ds(at, 1), :], (8, LANES))
-                    third = jnp.where(second, 0, (three >> shift) & 127).astype(jnp.float32)
-                pieces.append(jnp.concatenate([both, third], 0).astype(jnp.bfloat16))
-            table = jnp.concatenate([jnp.concatenate(highs, 1), jnp.concatenate(lows, 1)], 0)
+                    parts += [split(masked, at, masked, at + 1), empty]
+                pieces.append(jnp.concatenate(parts, 0).astype(jnp.bfloat16))
             part = lax.dot_general(
                 jnp.concatenate(pieces, 1),
-                table,
-                (((1,), (1,)), ((), ())),
+                jnp.concatenate(tables, 0),
+                (((1,), (0,)), ((), ())),
                 preferred_element_type=jnp.float32,
-            )
-            total = reduce_mod(total + part.astype(jnp.int32))
+            ).astype(jnp.int32)
+            if share:
+                total = reduce_mod(total + part)
+            else:
+                total = jnp.concatenate([reduce_mod(total[:16] + part), total[16:]], 0)
         return total
 
     units = blocks * per_block
@@ -366,7 +369,7 @@
             )
         return total
 
-    total = jnp.zeros((16, LANES), jnp.int32)
+    total = jnp.zeros((32, 2 * LANES), jnp.int32)
     for i in range(bits):
 
         def turn(h, total, i=i):
@@ -411,7 +414,11 @@
         total = lax.fori_loop(0, STREAMS, turn, total)
 
     flag_copy.wait()
-    total = reduce_mod(total * 32 + pltpu.roll(total, checks, 1))
+    total = reduce_mod(total[:, :LANES] * 32 + total[:, LANES:])
+    moved = pltpu.roll(total, checks, 1)
+    pair = total[0:8] + moved[8:16]
+    whole = total[16:24] + pltpu.roll(moved[16:24], 4, 0)
+    total = reduce_mod(jnp.concatenate([pair, whole], 0))
 
     def combine(r):
         high = reduce_mod(total[r + 2 : r + 3] * 128 + total[r + 1 : r + 2])
@@ -479,7 +486,7 @@
         scratch_shapes=[
             pltpu.VMEM((rows, LANES), jnp.int32),
             pltpu.VMEM((rows, LANES), jnp.int32),
-            pltpu.VMEM((checks, LANES), jnp.int32),
+            pltpu.VMEM((LANES, LANES), jnp.int32),
             pltpu.VMEM((block, LANES), jnp.int32),
             pltpu.VMEM((blocks * swap_rows, LANES), jnp.int32),
             pltpu.VMEM((blocks * swap_rows, LANES), jnp.int32),

time: 61.3 us -> 61 us (level)
  no operation moved by 1% of the time
where the time goes in v5:
time: 61 us; the launch traced here: 60.8 us
  Pallas kernels  59.5 us (98%)
  between operations  1.29 us (2%)
    pallas_call x1, Pallas kernels, aggregate_and_project(): pl.pallas_call(functools.partial(aggregate_kernel, clients, length), in_s...  57.6 us
    pallas_call x1, Pallas kernels, finish(): pl.pallas_call(functools.partial(finish_kernel, clients), grid=(STREAMS,)...  1.94 us

profile of v5, /device:TPU:0, one launch (start us, length us, event | category | flops | bytes accessed | tf_op | source)
XLA Modules:
  0.0 60.8 jit_solution(4370785646700899397)
XLA Ops:
  1.3 57.6 %aggregate_and_project.1 = (s32[2816,128]{1,0:T(8,128)S(1)}, s32[1,128]{1,0:T(1,128)S(1)}) custom-call(s32[1]{0:T(128)S(6)} %copy.7.alive_ref, s32[64]{0:T(128)} %seeds_ref.1, s32[4096,128]{1,0:T(8,128)} %bitcast.4, s32[4096,128]{1,0:T(8,128)} %bitcast.5), custom_call_target="tpu_custom_call" | custom-call | tf_op jit(solution)/shard_map/aggregate_and_project/pallas_call | solution.py:478
  58.9 1.9 %finish.1 = (s32[4096,128]{1,0:T(8,128)}, s32[1,64]{1,0:T(1,128)}, s32[1,64]{1,0:T(1,128)}) custom-call(s32[2816,128]{1,0:T(8,128)S(1)} %get-tuple-element.8.packed, s32[1,128]{1,0:T(1,128)S(1)} %get-tuple-element.9.sums), custom_call_target="tpu_custom_call" | custom-call | tf_op jit(solution)/shard_map/finish/pallas_call | solution.py:538

commit v6 on v5

--- a/solution.py
+++ b/solution.py
@@ -11,7 +11,8 @@
 mask21 = 2097151
 LANES = 128
 STREAMS = 4
-AHEAD = 3
+AHEAD = 4
+SPARE = 2
 STRIDE = (LANES * 747796405 + 2147483648) % 4294967296 - 2147483648
 
 
@@ -356,7 +357,7 @@
         return first + (early - first) * a // actions
 
     def ag_stop(a):
-        return early + (units - early) * (a + 1) // (actions - STREAMS)
+        return early + (units - early) * (a + 1) // (actions - STREAMS + SPARE)
 
     def compute(lo, hi, total, kinds):
         if "plain" in kinds:
@@ -412,6 +413,10 @@
             return total
 
         total = lax.fori_loop(0, STREAMS, turn, total)
+
+    last = ag_stop(actions - STREAMS - 1)
+    kinds = ("share",) if last >= plain else ("plain", "share")
+    total = compute(last, units, total, kinds)
 
     flag_copy.wait()
     total = reduce_mod(total[:, :LANES] * 32 + total[:, LANES:])

time: 61 us -> 61 us (level)
  no operation moved by 1% of the time
where the time goes in v6:
time: 61 us; the launch traced here: 60.9 us
  Pallas kernels  59.6 us (98%)
  between operations  1.29 us (2%)
    pallas_call x1, Pallas kernels, aggregate_and_project(): pl.pallas_call(functools.partial(aggregate_kernel, clients, length), in_s...  57.6 us
    pallas_call x1, Pallas kernels, finish(): pl.pallas_call(functools.partial(finish_kernel, clients), grid=(STREAMS,)...  1.94 us

profile of v6, /device:TPU:0, one launch (start us, length us, event | category | flops | bytes accessed | tf_op | source)
XLA Modules:
  0.0 60.9 jit_solution(15204825733146635555)
XLA Ops:
  1.3 57.6 %aggregate_and_project.1 = (s32[2816,128]{1,0:T(8,128)S(1)}, s32[1,128]{1,0:T(1,128)S(1)}) custom-call(s32[1]{0:T(128)S(6)} %copy.7.alive_ref, s32[64]{0:T(128)} %seeds_ref.1, s32[4096,128]{1,0:T(8,128)} %bitcast.4, s32[4096,128]{1,0:T(8,128)} %bitcast.5), custom_call_target="tpu_custom_call" | custom-call | tf_op jit(solution)/shard_map/aggregate_and_project/pallas_call | solution.py:483
  58.9 1.9 %finish.1 = (s32[4096,128]{1,0:T(8,128)}, s32[1,64]{1,0:T(1,128)}, s32[1,64]{1,0:T(1,128)}) custom-call(s32[2816,128]{1,0:T(8,128)S(1)} %get-tuple-element.8.packed, s32[1,128]{1,0:T(1,128)S(1)} %get-tuple-element.9.sums), custom_call_target="tpu_custom_call" | custom-call | tf_op jit(solution)/shard_map/finish/pallas_call | solution.py:543

commit v7 on v5

--- a/solution.py
+++ b/solution.py
@@ -457,7 +457,7 @@
     near = rows_in[0]
     for n in range(1, 2 * shards):
         near = near + rows_in[n]
-    every = lax.fori_loop(2 * shards, devices, lambda n, t: t + rows_in[n], near)
+    every = jnp.sum(rows_in[...], axis=0)
     sums_out[...] = reduce_mod(jnp.where(left, every, near))
 
 

time: 61 us -> 60.9 us (level)
  no operation moved by 1% of the time
where the time goes in v7:
time: 60.9 us; the launch traced here: 60.7 us
  Pallas kernels  59.4 us (98%)
  between operations  1.29 us (2%)
    pallas_call x1, Pallas kernels, aggregate_and_project(): pl.pallas_call(functools.partial(aggregate_kernel, clients, length), in_s...  57.5 us
    pallas_call x1, Pallas kernels, finish(): pl.pallas_call(functools.partial(finish_kernel, clients), grid=(STREAMS,)...  1.94 us

profile of v7, /device:TPU:0, one launch (start us, length us, event | category | flops | bytes accessed | tf_op | source)
XLA Modules:
  0.0 60.7 jit_solution(4063188025619897389)
XLA Ops:
  1.3 57.5 %aggregate_and_project.1 = (s32[2816,128]{1,0:T(8,128)S(1)}, s32[1,128]{1,0:T(1,128)S(1)}) custom-call(s32[1]{0:T(128)S(6)} %copy.7.alive_ref, s32[64]{0:T(128)} %seeds_ref.1, s32[4096,128]{1,0:T(8,128)} %bitcast.4, s32[4096,128]{1,0:T(8,128)} %bitcast.5), custom_call_target="tpu_custom_call" | custom-call | tf_op jit(solution)/shard_map/aggregate_and_project/pallas_call | solution.py:478
  58.8 1.9 %finish.1 = (s32[4096,128]{1,0:T(8,128)}, s32[1,64]{1,0:T(1,128)}, s32[1,64]{1,0:T(1,128)}) custom-call(s32[2816,128]{1,0:T(8,128)S(1)} %get-tuple-element.8.packed, s32[1,128]{1,0:T(1,128)S(1)} %get-tuple-element.9.sums), custom_call_target="tpu_custom_call" | custom-call | tf_op jit(solution)/shard_map/finish/pallas_call | solution.py:538
